TPU v7x, 32 devices: a whole 2x2x4 slice. The times are simulated.
32 devices in a mesh: grp: 4 (over z), cand: 8 (over y, x, core).
Axes of the slice: x: 2, y: 2, z: 4, core: 2. Of those that a mesh axis runs over, the one named last changes fastest.
Arguments:
- embeddings: bfloat16 [96, 1024, 1024], P('grp', 'cand'), may hold values from -6 to 6
- hidden_weight: bfloat16 [2048, 1024], P('cand'), may hold values from -0.1875 to 0.1875
- score_weight: bfloat16 [2048], replicated, may hold values from -0.5 to 0.5
- relevance: int32 [96, 1024], P('grp', 'cand'), may hold values from 0 to 4
- rank_pos: int32 [96, 1024], P('grp', 'cand'), may hold values from 0 to 1023, as said below
- ideal_dcg: float32 [96], P('grp'), may hold values from 32 to 128
Outputs:
- grad_hidden: float32 [2048, 1024], P('cand')
- lambdas: float32 [96, 1024], P('grp', 'cand')
Inputs may be any that keep to these rules, and one draw needn't show every extreme that they name: `rank_pos`: in each group the rank positions are a permutation of 0 to 1023.
All inputs are finite; a program needn't handle non-finite values.
Results may differ from a plain program's by a relative error of at most 0.006.
Values may be sent and summed in bfloat16 or wider, within the bound.
A program may use at most 64 MiB of HBM per device.

v0:
```python
import jax
import jax.numpy as jnp
from jax import lax
from jax.sharding import PartitionSpec as P

EPS = 1e-06


def pair_lambdas(own_score, own_gain, own_disc, far_score, far_gain, far_disc, ideal):
    gain_diff = far_gain[..., None, :] - own_gain[..., :, None]
    toward = jnp.sign(gain_diff)
    weight = (
        jnp.abs(gain_diff)
        * jnp.abs(far_disc[..., None, :] - own_disc[..., :, None])
        / ideal[..., None, None]
    )
    margin = own_score[..., :, None] - far_score[..., None, :]
    return jnp.sum(weight * toward * jax.nn.sigmoid(toward * margin), axis=-1)


def gain_of(labels):
    return jnp.exp2(labels.astype(jnp.float32)) - 1.0


def discount_of(positions):
    return 1.0 / jnp.log2(2.0 + positions.astype(jnp.float32))


def per_device(embeddings, hidden_weight, score_weight, relevance, rank_pos, ideal_dcg):
    grp_count, local, width = embeddings.shape
    cand_rows = embeddings.reshape(grp_count * local, width)
    pre_act = lax.dot_general(
        cand_rows,
        lax.all_gather(hidden_weight, "cand", axis=0, tiled=True),
        (((1,), (1,)), ((), ())),
        preferred_element_type=jnp.float32,
    )
    acts, pull = jax.vjp(jax.nn.gelu, pre_act)
    scores = jnp.dot(
        acts.astype(jnp.bfloat16), score_weight, preferred_element_type=jnp.float32
    ).reshape(grp_count, local)
    gain_vals = gain_of(relevance)
    discount = discount_of(rank_pos)
    lambdas = pair_lambdas(
        scores,
        gain_vals,
        discount,
        lax.all_gather(scores, "cand", axis=1, tiled=True),
        lax.all_gather(gain_vals, "cand", axis=1, tiled=True),
        lax.all_gather(discount, "cand", axis=1, tiled=True),
        ideal_dcg,
    )
    upstream = (
        lambdas.reshape(grp_count * local)[:, None] * score_weight.astype(jnp.float32)[None, :]
    )
    grad_pre = pull(upstream)[0].astype(jnp.bfloat16)
    owned = lax.psum_scatter(
        lax.dot_general(
            grad_pre, cand_rows, (((0,), (0,)), ((), ())), preferred_element_type=jnp.float32
        ).astype(jnp.bfloat16),
        "cand",
        scatter_dimension=0,
        tiled=True,
    ).astype(jnp.float32)
    summed = lax.psum(owned, "grp")
    squares = lax.psum(jnp.sum(summed * summed), "cand")
    entries = summed.shape[0] * summed.shape[1] * lax.axis_size("cand")
    scale = lax.rsqrt(squares / entries + EPS)
    return (summed * scale, lambdas)


def solution(mesh):
    return jax.shard_map(
        per_device,
        mesh=mesh,
        in_specs=(
            P("grp", "cand", None),
            P("cand", None),
            P(),
            P("grp", "cand"),
            P("grp", "cand"),
            P("grp"),
        ),
        out_specs=(P("cand", None), P("grp", "cand")),
        check_vma=False,
    )
```

profile of v0, /device:TPU:0, one launch (start us, length us, event | category | flops | bytes accessed | tf_op | source)
XLA Modules:
  0.0 254.7 jit_solution(1957202030902142692)
XLA Ops:
  7.2 0.0 all-gather.2.cloned.1.call-start
  7.2 0.7 all-gather.2.cloned.1.call-update
  7.9 0.0 reduce-scatter.2.cloned.1.call-start
  7.9 0.7 reshape.18
  8.6 0.7 convert_element_type.24
  9.3 0.7 exponential_add_fusion
  10.0 10.7 %all_gather.12 = f32[24,1024]{1,0:T(8,128)S(1)} all-gather(f32[24,128]{1,0:T(8,128)S(1)} %exponential_add_fusion), channel_id=1, replica_groups=mesh['grp'=4,'cand'=8] {'cand'}, dimensions={1}, use_global_device_ids=true | all-gather | bytes 110592 | tf_op jit(solution)/shard_map/all_gather | solution.py:49
  20.7 0.7 multiply_divide_fusion
  21.5 9.5 %all_gather.13 = f32[24,1024]{1,0:T(8,128)S(1)} all-gather(f32[24,128]{1,0:T(8,128)S(1)} %multiply_divide_fusion), channel_id=1, replica_groups=mesh['grp'=4,'cand'=8] {'cand'}, dimensions={1}, use_global_device_ids=true | all-gather | bytes 110592 | tf_op jit(solution)/shard_map/all_gather | solution.py:50
  31.0 18.5 %all-gather.2.cloned.1.call-done = bf16[2048,1024]{1,0:T(8,128)(2,1)} async-done(((bf16[256,1024]{1,0:T(8,128)(2,1)}), bf16[2048,1024]{1,0:T(8,128)(2,1)}) %all-gather.2.cloned.1.call-update) | async-done | bytes 4194320 | tf_op jit(solution)/shard_map/all_gather | solution.py:34
  49.5 19.7 %fusion.36 = f32[3072,2048]{1,0:T(8,128)} fusion(bf16[3072,1024]{1,0:T(8,128)(2,1)} %bitcast.11, bf16[2048,1024]{1,0:T(8,128)(2,1)} %all-gather.2.cloned.1.call-done), kind=kOutput, calls=%fused_computation.44 | convolution fusion | flops 12884901888 | bytes 35651584 | tf_op jit(solution)/shard_map/dot_general | solution.py:32
  69.1 0.0 copy-start
  69.1 11.9 %fusion.20 = f32[1,3072]{1,0:T(1,128)S(1)} fusion(bf16[2048,1]{0,1:T(2,128)(2,1)S(1)} %reshape.18, f32[3072,2048]{1,0:T(8,128)} %fusion.36), kind=kOutput, calls=%fused_computation.27 | convolution fusion | flops 69206016 | bytes 25182208 | tf_op jit(solution)/shard_map/dot_general | solution.py:39
  81.1 9.1 %all_gather.15 = f32[24,1024]{1,0:T(8,128)S(1)} all-gather(f32[24,128]{1,0:T(8,128)S(1)} %bitcast.9), channel_id=1, replica_groups=mesh['grp'=4,'cand'=8] {'cand'}, dimensions={1}, use_global_device_ids=true | all-gather | bytes 110592 | tf_op jit(solution)/shard_map/all_gather | solution.py:48
  90.2 0.0 copy-done
  90.2 11.2 %fusion.13 = f32[24,128]{1,0:T(8,128)S(1)} fusion(f32[24,1024]{1,0:T(8,128)S(1)} %all_gather.15, f32[24,128]{1,0:T(8,128)S(1)} %bitcast.10, f32[24]{0:T(128)S(1)} %copy-done, f32[24,128]{1,0:T(8,128)S(1)} %multiply_divide_fusion, f32[24,1024]{1,0:T(8,128)S(1)} %all_gather.13, f32[24,128]{1,0:T(8,128)S(1)} %exponential_add_fusion, f32[24,1024]{1,0:T(8,128)S(1)} %all_gather.12), kind=kLoop, calls=%fused_computation.20 | loop fusion | flops 47182848 | bytes 344160 | tf_op jit(solution)/shard_map/reduce_sum | solution.py:18
  101.4 0.0 copy-start.1
  101.4 35.9 %fusion.23 = bf16[2048,1024]{1,0:T(8,128)(2,1)} fusion(bf16[3072,1024]{1,0:T(8,128)(2,1)} %bitcast.12, f32[3072,2048]{1,0:T(8,128)} %fusion.36, f32[2048]{0:T(1024)S(1)} %convert_element_type.24, f32[3072]{0:T(1024)S(1)} %bitcast.13), kind=kOutput, calls=%fused_computation.29 | convolution fusion | flops 13019119616 | bytes 35672064 | tf_op jit(solution)/shard_map/dot_general | solution.py:58
  137.3 0.0 copy-done.1
  137.3 0.0 reduce-scatter.2.cloned.1.call-update
  137.4 51.3 %reduce-scatter.2.cloned.1.call-done = bf16[256,1024]{1,0:T(8,128)(2,1)} async-done(((bf16[2048,1024]{1,0:T(8,128)(2,1)}), bf16[256,1024]{1,0:T(8,128)(2,1)}) %reduce-scatter.2.cloned.1.call-update) | async-done | bytes 524304 | tf_op jit(solution)/shard_map/reduce_scatter | solution.py:57
  188.7 44.2 %all-reduce.1 = f32[256,1024]{1,0:T(8,128)S(1)} all-reduce(bf16[256,1024]{1,0:T(8,128)(2,1)} %reduce-scatter.2.cloned.1.call-done), channel_id=1, replica_groups=mesh['grp'=4,'cand'=8] {'grp'}, use_global_device_ids=true, to_apply=%region_2.0 | all-reduce | flops 262144 | bytes 1572864 | tf_op jit(solution)/shard_map/psum | solution.py:65
  232.9 0.9 multiply_reduce_fusion
  233.8 12.4 %psum.15 = f32[]{:T(128)} all-reduce(f32[]{:T(128)} %multiply_reduce_fusion), channel_id=1, replica_groups=mesh['grp'=4,'cand'=8] {'cand'}, use_global_device_ids=true, to_apply=%region_4.0 | all-reduce | flops 1 | bytes 8 | tf_op jit(solution)/shard_map/psum | solution.py:66
  246.9 1.0 broadcast_multiply_fusion
Async XLA Ops:
  7.2 42.3 %all-gather.2.cloned.1.call-start = ((), (), s32[]{:S(2)}) async-start(), calls=%async_computation.1 | async-start | bytes 4718592 | tf_op jit(solution)/shard_map/all_gather | solution.py:34
  7.9 180.8 %reduce-scatter.2.cloned.1.call-start = ((), (), s32[]{:S(2)}) async-start(), calls=%async_computation.2 | async-start | bytes 4718592 | tf_op jit(solution)/shard_map/reduce_scatter | solution.py:57
  69.1 21.1 %copy-start = (f32[24]{0:T(128)S(1)}, f32[24]{0:T(128)}, u32[]{:S(2)}) copy-start(f32[24]{0:T(128)} %param.11) | copy-start | bytes 292
  101.4 36.0 %copy-start.1 = (f32[24,128]{1,0:T(8,128)}, f32[24,128]{1,0:T(8,128)S(1)}, u32[]{:S(2)}) copy-start(f32[24,128]{1,0:T(8,128)S(1)} %fusion.13) | copy-start | bytes 36868
Sparse Core Ops, SparseCore 0:
  9.9 39.5 all-gather.1
  137.5 51.1 reduce-scatter.1
where the time goes:
time: 255 us
  blocking collectives  86 us (34%)
  waiting for transfers between devices  70.5 us (28%)
  matrix products  67.5 us (26%)
  other arithmetic  15.2 us (6%)
  between operations  14.8 us (6%)
    reduce_scatter x1, waiting for transfers between devices, per_device(): lax.psum_scatter(lax.dot_general(grad_pre, cand_rows, (((0,), (0,)), ((),...  51.3 us
    psum x1, blocking collectives, per_device(): summed = lax.psum(owned, 'grp')  44.2 us
    dot_general x1, matrix products, per_device(): lax.dot_general(grad_pre, cand_rows, (((0,), (0,)), ((), ())), preferred_...  35.9 us
    dot_general x1, matrix products, per_device(): lax.dot_general(cand_rows, lax.all_gather(hidden_weight, 'cand', axis=0,...  19.7 us
    all_gather x1, waiting for transfers between devices, per_device(): lax.all_gather(hidden_weight, 'cand', axis=0, tiled=True)  18.5 us
    psum x1, blocking collectives, per_device(): squares = lax.psum(jnp.sum(summed * summed), 'cand')  12.4 us
    dot_general x1, matrix products, per_device(): jnp.dot(acts.astype(jnp.bfloat16), score_weight, preferred_element_type=j...  11.9 us
    reduce_sum x1, other arithmetic, pair_lambdas(): return jnp.sum(weight * toward * jax.nn.sigmoid(toward * margin), axis=-1)  11.2 us
  transfers between devices with their start and end apart: 2, of which 2 were waited for; matrix products, arithmetic and copies ran while one was open for 1% of the time, Pallas kernels for 0%

commit v1 on v0

--- a/solution.py
+++ b/solution.py
@@ -62,7 +62,11 @@
         scatter_dimension=0,
         tiled=True,
     ).astype(jnp.float32)
-    summed = lax.psum(owned, "grp")
+    size = lax.axis_size("grp")
+    summed, reach = (owned, 1)
+    while reach < size:
+        summed = summed + lax.ppermute(summed, "grp", [(i, i ^ reach) for i in range(size)])
+        reach = 2 * reach
     squares = lax.psum(jnp.sum(summed * summed), "cand")
     entries = summed.shape[0] * summed.shape[1] * lax.axis_size("cand")
     scale = lax.rsqrt(squares / entries + EPS)

time: 255 us -> 286 us (1.12)
  waiting for transfers between devices: 70.5 us -> 139 us
  blocking collectives: 86 us -> 41.9 us
  starting transfers between devices: 0.08 us -> 4.11 us
    ppermute x0 -> x2, waiting for transfers between devices: none -> 68.1 us  [per_device(): lax.ppermute(summed, 'grp', [(i, i ^ reach) for i in range(size)])]
    psum x1 -> x0, blocking collectives: 44.2 us -> none  [per_device(): summed = lax.psum(owned, 'grp')]
    ppermute x0 -> x2, starting transfers between devices: none -> 4.03 us  [per_device(): lax.ppermute(summed, 'grp', [(i, i ^ reach) for i in range(size)])]
  transfers between devices with their start and end apart: 2 -> 4, of which waited for: 2 -> 4; matrix products, arithmetic and copies ran while one was open for 1% -> 1% of each run, Pallas kernels for 0% -> 0%
where the time goes in v1:
time: 286 us; the launch traced here: 285 us
  waiting for transfers between devices  139 us (49%)
  matrix products  67.5 us (24%)
  blocking collectives  41.9 us (15%)
  other arithmetic  17.7 us (6%)
  between operations  14.8 us (5%)
  starting transfers between devices  4.11 us (1%)
    ppermute x2, waiting for transfers between devices, per_device(): lax.ppermute(summed, 'grp', [(i, i ^ reach) for i in range(size)])  68.1 us
    reduce_scatter x1, waiting for transfers between devices, per_device(): lax.psum_scatter(lax.dot_general(grad_pre, cand_rows, (((0,), (0,)), ((),...  51.3 us
    dot_general x1, matrix products, per_device(): lax.dot_general(grad_pre, cand_rows, (((0,), (0,)), ((), ())), preferred_...  35.9 us
    dot_general x1, matrix products, per_device(): lax.dot_general(cand_rows, lax.all_gather(hidden_weight, 'cand', axis=0,...  19.7 us
    all_gather x1, waiting for transfers between devices, per_device(): lax.all_gather(hidden_weight, 'cand', axis=0, tiled=True)  18.5 us
    psum x1, blocking collectives, per_device(): squares = lax.psum(jnp.sum(summed * summed), 'cand')  12.6 us
    dot_general x1, matrix products, per_device(): jnp.dot(acts.astype(jnp.bfloat16), score_weight, preferred_element_type=j...  11.9 us
    reduce_sum x1, other arithmetic, pair_lambdas(): return jnp.sum(weight * toward * jax.nn.sigmoid(toward * margin), axis=-1)  11.2 us
  transfers between devices with their start and end apart: 4, of which 4 were waited for; matrix products, arithmetic and copies ran while one was open for 1% of the time, Pallas kernels for 0%

profile of v1, /device:TPU:0, one launch (start us, length us, event | category | flops | bytes accessed | tf_op | source)
XLA Modules:
  0.0 285.3 jit_solution(2072965509809762156)
XLA Ops:
  7.2 0.0 all-gather.2.cloned.1.call-start
  7.2 0.7 all-gather.2.cloned.1.call-update
  7.9 0.0 reduce-scatter.2.cloned.1.call-start
  7.9 0.7 reshape.18
  8.6 0.7 convert_element_type.24
  9.3 0.7 exponential_add_fusion
  10.0 10.7 %all_gather.12 = f32[24,1024]{1,0:T(8,128)S(1)} all-gather(f32[24,128]{1,0:T(8,128)S(1)} %exponential_add_fusion), channel_id=1, replica_groups=mesh['grp'=4,'cand'=8] {'cand'}, dimensions={1}, use_global_device_ids=true | all-gather | bytes 110592 | tf_op jit(solution)/shard_map/all_gather | solution.py:49
  20.7 0.7 multiply_divide_fusion
  21.5 9.5 %all_gather.13 = f32[24,1024]{1,0:T(8,128)S(1)} all-gather(f32[24,128]{1,0:T(8,128)S(1)} %multiply_divide_fusion), channel_id=1, replica_groups=mesh['grp'=4,'cand'=8] {'cand'}, dimensions={1}, use_global_device_ids=true | all-gather | bytes 110592 | tf_op jit(solution)/shard_map/all_gather | solution.py:50
  31.0 18.5 %all-gather.2.cloned.1.call-done = bf16[2048,1024]{1,0:T(8,128)(2,1)} async-done(((bf16[256,1024]{1,0:T(8,128)(2,1)}), bf16[2048,1024]{1,0:T(8,128)(2,1)}) %all-gather.2.cloned.1.call-update) | async-done | bytes 4194320 | tf_op jit(solution)/shard_map/all_gather | solution.py:34
  49.5 19.7 %fusion.36 = f32[3072,2048]{1,0:T(8,128)} fusion(bf16[3072,1024]{1,0:T(8,128)(2,1)} %bitcast.11, bf16[2048,1024]{1,0:T(8,128)(2,1)} %all-gather.2.cloned.1.call-done), kind=kOutput, calls=%fused_computation.45 | convolution fusion | flops 12884901888 | bytes 35651584 | tf_op jit(solution)/shard_map/dot_general | solution.py:32
  69.1 0.0 copy-start
  69.1 11.9 %fusion.20 = f32[1,3072]{1,0:T(1,128)S(1)} fusion(bf16[2048,1]{0,1:T(2,128)(2,1)S(1)} %reshape.18, f32[3072,2048]{1,0:T(8,128)} %fusion.36), kind=kOutput, calls=%fused_computation.27 | convolution fusion | flops 69206016 | bytes 25182208 | tf_op jit(solution)/shard_map/dot_general | solution.py:39
  81.1 9.1 %all_gather.15 = f32[24,1024]{1,0:T(8,128)S(1)} all-gather(f32[24,128]{1,0:T(8,128)S(1)} %bitcast.9), channel_id=1, replica_groups=mesh['grp'=4,'cand'=8] {'cand'}, dimensions={1}, use_global_device_ids=true | all-gather | bytes 110592 | tf_op jit(solution)/shard_map/all_gather | solution.py:48
  90.2 0.0 copy-done
  90.2 11.2 %fusion.13 = f32[24,128]{1,0:T(8,128)S(1)} fusion(f32[24,1024]{1,0:T(8,128)S(1)} %all_gather.15, f32[24,128]{1,0:T(8,128)S(1)} %bitcast.10, f32[24]{0:T(128)S(1)} %copy-done, f32[24,128]{1,0:T(8,128)S(1)} %multiply_divide_fusion, f32[24,1024]{1,0:T(8,128)S(1)} %all_gather.13, f32[24,128]{1,0:T(8,128)S(1)} %exponential_add_fusion, f32[24,1024]{1,0:T(8,128)S(1)} %all_gather.12), kind=kLoop, calls=%fused_computation.20 | loop fusion | flops 47182848 | bytes 344160 | tf_op jit(solution)/shard_map/reduce_sum | solution.py:18
  101.4 0.0 copy-start.1
  101.4 35.9 %fusion.23 = bf16[2048,1024]{1,0:T(8,128)(2,1)} fusion(bf16[3072,1024]{1,0:T(8,128)(2,1)} %bitcast.12, f32[3072,2048]{1,0:T(8,128)} %fusion.36, f32[2048]{0:T(1024)S(1)} %convert_element_type.24, f32[3072]{0:T(1024)S(1)} %bitcast.13), kind=kOutput, calls=%fused_computation.29 | convolution fusion | flops 13019119616 | bytes 35672064 | tf_op jit(solution)/shard_map/dot_general | solution.py:58
  137.3 0.0 copy-done.1
  137.3 0.0 reduce-scatter.2.cloned.1.call-update
  137.4 51.3 %reduce-scatter.2.cloned.1.call-done = bf16[256,1024]{1,0:T(8,128)(2,1)} async-done(((bf16[2048,1024]{1,0:T(8,128)(2,1)}), bf16[256,1024]{1,0:T(8,128)(2,1)}) %reduce-scatter.2.cloned.1.call-update) | async-done | bytes 524304 | tf_op jit(solution)/shard_map/reduce_scatter | solution.py:57
  188.7 1.1 convert_element_type.27
  189.8 1.5 collective-permute-start
  191.4 23.2 %collective-permute-done = f32[256,1024]{1,0:T(8,128)S(1)} collective-permute-done((f32[256,1024]{1,0:T(8,128)S(1)}, f32[256,1024]{1,0:T(8,128)S(1)}, u32[]{:S(2)}, u32[]{:S(2)}) %collective-permute-start) | collective-permute-done | bytes 1048608 | tf_op jit(solution)/shard_map/ppermute | solution.py:68
  214.6 1.2 convert_add_fusion
  215.8 2.5 collective-permute-start.1
  218.3 44.8 %collective-permute-done.1 = f32[256,1024]{1,0:T(8,128)S(1)} collective-permute-done((f32[256,1024]{1,0:T(8,128)S(1)}, f32[256,1024]{1,0:T(8,128)S(1)}, u32[]{:S(2)}, u32[]{:S(2)}) %collective-permute-start.1) | collective-permute-done | bytes 1048608 | tf_op jit(solution)/shard_map/ppermute | solution.py:68
  263.1 1.0 multiply_reduce_fusion
  264.1 12.6 %psum.7 = f32[]{:T(128)} all-reduce(f32[]{:T(128)} %get-tuple-element.2), channel_id=1, replica_groups=mesh['grp'=4,'cand'=8] {'cand'}, use_global_device_ids=true, to_apply=%region_3.0 | all-reduce | flops 1 | bytes 8 | tf_op jit(solution)/shard_map/psum | solution.py:70
  277.4 1.0 broadcast_multiply_fusion
Async XLA Ops:
  7.2 42.3 %all-gather.2.cloned.1.call-start = ((), (), s32[]{:S(2)}) async-start(), calls=%async_computation.1 | async-start | bytes 4718592 | tf_op jit(solution)/shard_map/all_gather | solution.py:34
  7.9 180.8 %reduce-scatter.2.cloned.1.call-start = ((), (), s32[]{:S(2)}) async-start(), calls=%async_computation.2 | async-start | bytes 4718592 | tf_op jit(solution)/shard_map/reduce_scatter | solution.py:57
  69.1 21.1 %copy-start = (f32[24]{0:T(128)S(1)}, f32[24]{0:T(128)}, u32[]{:S(2)}) copy-start(f32[24]{0:T(128)} %param.11) | copy-start | bytes 292
  101.4 36.0 %copy-start.1 = (f32[24,128]{1,0:T(8,128)}, f32[24,128]{1,0:T(8,128)S(1)}, u32[]{:S(2)}) copy-start(f32[24,128]{1,0:T(8,128)S(1)} %fusion.13) | copy-start | bytes 36868
  189.8 24.8 %collective-permute-start = (f32[256,1024]{1,0:T(8,128)S(1)}, f32[256,1024]{1,0:T(8,128)S(1)}, u32[]{:S(2)}, u32[]{:S(2)}) collective-permute-start(f32[256,1024]{1,0:T(8,128)S(1)} %convert_element_type.27), channel_id=1, source_target_pairs={{0,8},{8,0},{16,24},{24,16},{1,9},{9,1},{17,25},{25,17},{2,10},{10... | collective-permute-start | bytes 3145736 | tf_op jit(solution)/shard_map/ppermute | solution.py:68
  215.8 47.3 %collective-permute-start.1 = (f32[256,1024]{1,0:T(8,128)S(1)}, f32[256,1024]{1,0:T(8,128)S(1)}, u32[]{:S(2)}, u32[]{:S(2)}) collective-permute-start(f32[256,1024]{1,0:T(8,128)S(1)} %convert_add_fusion), channel_id=1, source_target_pairs={{0,16},{8,24},{16,0},{24,8},{1,17},{9,25},{17,1},{25,9},{2,18},{10... | collective-permute-start | bytes 3145736 | tf_op jit(solution)/shard_map/ppermute | solution.py:68
Sparse Core Ops, SparseCore 0:
  9.9 39.5 all-gather.1
  137.5 51.1 reduce-scatter.1
